TPU v7x, 32 devices: a whole 2x2x4 slice. The times are simulated.
32 devices in a mesh: dp: 8 (over y, x, core), tensor: 4 (over z).
Axes of the slice: x: 2, y: 2, z: 4, core: 2. Of those that a mesh axis runs over, the one named last changes fastest.
Arguments:
- text: bfloat16 [8, 256, 5120], P('dp', None, 'tensor'), may hold values from -6 to 6
- prompts: bfloat16 [8, 100, 5120], P('dp', None, 'tensor'), may hold values from -6 to 6
- gain: float32 [5120], replicated, may hold values from 0.1 to 1.9
- w_query: bfloat16 [5120, 3072], P(None, 'tensor'), may hold values from -0.069877124 to 0.069877124, as said below
- w_key: bfloat16 [5120, 3072], P(None, 'tensor'), may hold values from -1.2577882 to 1.2577882, as said below
- w_value: bfloat16 [5120, 3072], P(None, 'tensor'), may hold values from -0.078125 to 0.078125
- cotangent: bfloat16 [8, 356, 3072], P('dp', None, 'tensor'), may hold values from -6 to 6
- task_of: int32 [8], replicated, may hold values from 0 to 7, as said below
- lengths: int32 [8], replicated, may hold values from 1 to 256, as said below
- slot: int32 [8], replicated, may hold values from 0 to 7, as said below
Outputs:
- attn_out: bfloat16 [8, 356, 3072], P('dp', None, 'tensor')
- prompt_grad: float32 [8, 100, 5120], P('dp', None, 'tensor')
Inputs may be any that keep to these rules, and one draw needn't show every extreme that they name: `task_of`: nondecreasing along the source order. `lengths`: some example has exactly 256 text tokens; rows of an example beyond its length are padding. `slot`: a permutation of 0 to 7; position s lies on index s // 1 of dp. `w_query`: entries of order 5120 ** -0.5. `w_key`: entries of order 5120 ** -0.5 or larger.
All inputs are finite; a program needn't handle non-finite values.
Results may differ from a plain program's by a relative error of at most 0.0082.
Values may be sent and summed in bfloat16 or wider, within the bound.
A program may use at most 128 MiB of HBM per device.

v0:
```python
import functools
import math

import jax
import jax.numpy as jnp
import numpy as np
from jax import lax
from jax.experimental import pallas as pl
from jax.experimental.pallas import tpu as pltpu
from jax.sharding import PartitionSpec as P

HD = 128


def rope_tables(row_count):
    half_dim = HD // 2
    frequency = 10000.0 ** (-jnp.arange(half_dim, dtype=jnp.float32) / half_dim)
    angle_table = jnp.arange(row_count, dtype=jnp.float32)[:, None] * frequency[None, :]
    return (jnp.cos(angle_table), jnp.sin(angle_table))


def rotate(vectors, cosine_table, sine_table):
    half_dim = vectors.shape[-1] // 2
    first_half = vectors[..., :half_dim]
    second_half = vectors[..., half_dim:]
    cosine_b = cosine_table[:, None, :]
    sine_b = sine_table[:, None, :]
    return jnp.concatenate(
        [
            first_half * cosine_b - second_half * sine_b,
            second_half * cosine_b + first_half * sine_b,
        ],
        axis=-1,
    )


def unrotate(vectors, cosine_table, sine_table):
    half_dim = vectors.shape[-1] // 2
    first_half = vectors[..., :half_dim]
    second_half = vectors[..., half_dim:]
    cosine_b = cosine_table[:, None, :]
    sine_b = sine_table[:, None, :]
    return jnp.concatenate(
        [
            first_half * cosine_b + second_half * sine_b,
            second_half * cosine_b - first_half * sine_b,
        ],
        axis=-1,
    )


def transpose_product(grad_low, matrix):
    return lax.dot_general(
        grad_low, matrix, (((1,), (1,)), ((), ())), preferred_element_type=jnp.float32
    )


def attention_window(full_rows, gain, w_query, w_key, w_value, cotangent, valid_rows, prompt_len):
    batch_size, row_count, model_width = full_rows.shape
    head_count = w_query.shape[1] // HD
    wide_rows = full_rows.astype(jnp.float32)
    inv_rms = lax.rsqrt(jnp.mean(wide_rows * wide_rows, axis=-1) + 1e-05)
    normed = (
        (wide_rows * inv_rms[..., None] * gain)
        .astype(jnp.bfloat16)
        .reshape(batch_size * row_count, model_width)
    )
    cosine_table, sine_table = rope_tables(row_count)

    def project(matrix):
        return jnp.dot(normed, matrix, preferred_element_type=jnp.float32).reshape(
            batch_size, row_count, head_count, HD
        )

    queries = rotate(project(w_query), cosine_table, sine_table).astype(jnp.bfloat16)
    key_rows = rotate(project(w_key), cosine_table, sine_table).astype(jnp.bfloat16)
    value_rows = project(w_value).astype(jnp.bfloat16)
    score_scale = 1.0 / math.sqrt(HD)
    scores = (
        jnp.einsum("erhd,ekhd->ehrk", queries, key_rows, preferred_element_type=jnp.float32)
        * score_scale
    )
    rows_at = jnp.arange(row_count, dtype=jnp.int32)
    row_limit = prompt_len + valid_rows
    allowed = (rows_at[None, None, :] <= rows_at[None, :, None]) & (
        rows_at[None, None, :] < row_limit[:, None, None]
    )
    allowed = allowed[:, None]
    scores = jnp.where(allowed, scores, -1e30)
    row_peak = jnp.max(scores, axis=-1, keepdims=True)
    weights = jnp.where(allowed, jnp.exp(scores - row_peak), 0.0)
    probability = weights / jnp.sum(weights, axis=-1, keepdims=True)
    probs_low = probability.astype(jnp.bfloat16)
    live_rows = rows_at[None, :] < row_limit[:, None]
    mixed_rows = jnp.einsum(
        "ehrk,ekhd->erhd", probs_low, value_rows, preferred_element_type=jnp.float32
    )
    mixed_rows = jnp.where(live_rows[:, :, None, None], mixed_rows, 0.0)
    output = mixed_rows.reshape(batch_size, row_count, head_count * HD).astype(jnp.bfloat16)
    upstream = jnp.where(
        live_rows[:, :, None, None], cotangent.reshape(batch_size, row_count, head_count, HD), 0.0
    )
    grad_prob = jnp.einsum(
        "erhd,ekhd->ehrk", upstream, value_rows, preferred_element_type=jnp.float32
    )
    row_delta = jnp.sum(probability * grad_prob, axis=-1, keepdims=True)
    grad_score = (probability * (grad_prob - row_delta)).astype(jnp.bfloat16)
    grad_query = (
        jnp.einsum(
            "ehrk,ekhd->erhd",
            grad_score[:, :, :prompt_len, :],
            key_rows,
            preferred_element_type=jnp.float32,
        )
        * score_scale
    )
    grad_key = (
        jnp.einsum(
            "ehrk,erhd->ekhd",
            grad_score[:, :, :, :prompt_len],
            queries,
            preferred_element_type=jnp.float32,
        )
        * score_scale
    )
    grad_value = jnp.einsum(
        "ehrk,erhd->ekhd",
        probs_low[:, :, :, :prompt_len],
        upstream,
        preferred_element_type=jnp.float32,
    )
    cosine_lead = cosine_table[:prompt_len]
    sine_lead = sine_table[:prompt_len]
    flat_rows = batch_size * prompt_len
    grad_query = (
        unrotate(grad_query, cosine_lead, sine_lead)
        .astype(jnp.bfloat16)
        .reshape(flat_rows, head_count * HD)
    )
    grad_key = (
        unrotate(grad_key, cosine_lead, sine_lead)
        .astype(jnp.bfloat16)
        .reshape(flat_rows, head_count * HD)
    )
    grad_value = grad_value.astype(jnp.bfloat16).reshape(flat_rows, head_count * HD)
    grad_normed = (
        transpose_product(grad_query, w_query)
        + transpose_product(grad_key, w_key)
        + transpose_product(grad_value, w_value)
    )
    grad_normed = grad_normed.reshape(batch_size, prompt_len, model_width) * gain
    prompt_rows = wide_rows[:, :prompt_len]
    prompt_inv = inv_rms[:, :prompt_len, None]
    grad_rows = prompt_inv * grad_normed - prompt_rows * prompt_inv**3 * jnp.mean(
        grad_normed * prompt_rows, axis=-1, keepdims=True
    )
    return (output, grad_rows)


def on_device(text, prompts, gain, w_query, w_key, w_value, cotangent, task_of, lengths, slot):
    dp_count = lax.axis_size("dp")
    my_index = lax.axis_index("dp")
    ex_dev = text.shape[0]
    task_dev = prompts.shape[0]
    prompt_len = prompts.shape[1]
    example_count = slot.shape[0]
    task_count = task_dev * dp_count
    places = jnp.arange(example_count, dtype=jnp.int32)
    matching = slot[None, :] == places[:, None]
    task_slot = jnp.sum(jnp.where(matching, task_of[None, :], 0), axis=1)
    length_slot = jnp.sum(jnp.where(matching, lengths[None, :], 0), axis=1)
    first_place = my_index * ex_dev
    my_lengths = lax.dynamic_slice_in_dim(length_slot, first_place, ex_dev)
    task_ids = jnp.arange(task_count, dtype=jnp.int32)
    spread_text, spread_prompts = (
        lax.all_to_all(text, "dp", split_axis=2, concat_axis=0, tiled=True),
        lax.all_to_all(prompts, "dp", split_axis=2, concat_axis=0, tiled=True),
    )
    taking = matching.astype(jnp.bfloat16)
    placed_text = jnp.einsum(
        "se,erc->src", taking, spread_text, preferred_element_type=jnp.bfloat16
    )
    choosing = (task_slot[:, None] == task_ids[None, :]).astype(jnp.bfloat16)
    placed_prompts = jnp.einsum(
        "st,tpc->spc", choosing, spread_prompts, preferred_element_type=jnp.bfloat16
    )
    placed = jnp.concatenate([placed_prompts, placed_text], axis=1)
    placed = placed.reshape(dp_count, ex_dev, placed.shape[1], placed.shape[2])
    local_rows = lax.all_to_all(placed, "dp", split_axis=0, concat_axis=3, tiled=True)[0]
    full_rows = lax.all_gather(local_rows, "tensor", axis=2, tiled=True)
    output, grad_part = attention_window(
        full_rows, gain, w_query, w_key, w_value, cotangent, my_lengths, prompt_len
    )
    grad_share = lax.psum_scatter(grad_part, "tensor", scatter_dimension=2, tiled=True)
    spread_grads = lax.all_to_all(grad_share, "dp", split_axis=2, concat_axis=0, tiled=True)
    collecting = (task_ids[:, None] == task_slot[None, :]).astype(jnp.float32)
    per_task = jnp.einsum("ts,spc->tpc", collecting, spread_grads, precision=lax.Precision.HIGHEST)
    prompt_grad = lax.all_to_all(per_task, "dp", split_axis=0, concat_axis=2, tiled=True)
    return (output, prompt_grad)


MESH = pl.DeviceIdType.MESH
PAD_POS = 1 << 20


def dot_nn(a, b):
    return jnp.dot(a, b, preferred_element_type=jnp.float32)


def dot_nt(a, b):
    return lax.dot_general(a, b, (((1,), (1,)), ((), ())), preferred_element_type=jnp.float32)


def dot_tn(a, b):
    return lax.dot_general(a, b, (((0,), (0,)), ((), ())), preferred_element_type=jnp.float32)


def step_kernel(
    p_len, slot_ref, task_ref, length_ref, inp_ref, gain_ref, cos_ref, sin_ref, posr_ref, posc_ref,
    cot_ref, wq_hbm, wk_hbm, wv_hbm, out_ref, grad_ref,
    w_ref, recv, send, full, squares, qkv, grads, inv_ref, acc, part, recvz, send1, recv1, send2, recv2,
    semw, sem1, sem2, semz, semq, semg, sem3, sem4,
):
    n, m = lax.axis_size("dp"), lax.axis_size("tensor")
    me, t = lax.axis_index("dp"), lax.axis_index("tensor")
    f32, bf16 = jnp.float32, jnp.bfloat16
    right, left = lax.rem(t + 1, m), lax.rem(t + m - 1, m)
    _, chunk, width = inp_ref.shape
    blocks, model_width, group = w_ref.shape
    per = blocks // 3
    rows = n * chunk
    lead = chunk // 3
    split = chunk - lead

    def pick(place, values):
        total = jnp.int32(0)
        for e in range(n):
            total = jnp.maximum(total, jnp.where(slot_ref[e] == place, values(e), 0))
        return total

    def source_of(place):
        return pick(place, lambda e: e)

    def task_at(place):
        return pick(place, lambda e: task_ref[e])

    def remote(src, dst, sems, device, needed=None):
        copy = pltpu.make_async_remote_copy(
            src_ref=src,
            dst_ref=dst,
            send_sem=sems[0],
            recv_sem=sems[1],
            device_id=device,
            device_id_type=MESH,
        )
        if needed is None:
            copy.start()
        else:
            pl.when(needed)(copy.start)
        return copy

    def holds(at):
        return at * lead < p_len

    loads = []
    for i, hbm in enumerate((wq_hbm, wk_hbm, wv_hbm)):
        for g in range(per):
            at = i * per + g
            load = pltpu.make_async_copy(
                hbm.at[:, g * group : (g + 1) * group], w_ref.at[at], semw.at[at]
            )
            load.start()
            loads.append(load)

    barrier = pltpu.get_barrier_semaphore()
    for k in range(1, n):
        pl.semaphore_signal(
            barrier, inc=1, device_id=(lax.rem(me + k, n), t), device_id_type=MESH
        )
    for k in range(1, m):
        pl.semaphore_signal(
            barrier, inc=1, device_id=(me, lax.rem(t + k, m)), device_id_type=MESH
        )
    pl.semaphore_wait(barrier, n + m - 2)

    first = []
    for k in range(1, n):
        peer = lax.rem(me + k, n)
        sems = (sem1.at[0, k], sem1.at[1, k])
        first.append(remote(inp_ref.at[peer], recv.at[me], sems, (peer, t)))
    recv[me] = inp_ref[me]
    for copy in first:
        copy.wait_recv()

    second = []
    for k in range(1, n):
        peer = lax.rem(me + k, n)
        send[k, :split] = recv[source_of(peer), :split]
        send[k, split:] = recv[task_at(peer), split:]
        sems = (sem2.at[0, k], sem2.at[1, k])
        second.append(remote(send.at[k], full.at[t, me], sems, (peer, t)))
    full[t, me, :split] = recv[source_of(me), :split]
    full[t, me, split:] = recv[task_at(me), split:]

    def hop(origin, k, distance, way):
        place = full.at[origin, lax.rem(me + n - k, n)]
        sems = (semz.at[0, way, distance, k], semz.at[1, way, distance, k])
        return remote(place, place, sems, (me, left if way else right))

    def reach(k, way):
        half = m // 2
        return half if way == k % 2 else m - 1 - half

    hops = {}
    for k in range(n):
        if k:
            second[k - 1].wait_recv()
        for way in (0, 1):
            hops[way, 1, k] = hop(t, k, 1, way)

    own = full[t].reshape(rows, width).astype(f32)
    square = jnp.sum(own * own, axis=1, keepdims=True)
    squares[0] = jnp.broadcast_to(square, (rows, 128)).T[:8]
    shared = []
    for k in range(1, m):
        peer = lax.rem(t + k, m)
        sems = (semq.at[0, k], semq.at[1, k])
        shared.append(remote(squares.at[0], squares.at[k], sems, (me, peer)))

    def origin_of(distance, way):
        return lax.rem(t + (m - distance if way == 0 else distance), m)

    def receive(distance):
        for k in range(n):
            for way in (0, 1):
                if distance <= reach(k, way):
                    hops[way, distance, k].wait_recv()
                    if distance < reach(k, way):
                        origin = origin_of(distance, way)
                        hops[way, distance + 1, k] = hop(origin, k, distance + 1, way)

    def project(origin, fresh):
        wide = full[origin].reshape(rows, width).astype(f32)
        normed = (wide * inv_ref[:, :1] * gain_ref[origin]).astype(bf16)
        deep = pl.ds(pl.multiple_of(origin * width, width), width)

        def body(b, carry):
            product = dot_nn(normed, w_ref[b, deep, :])
            qkv[b] = product if fresh else qkv[b] + product
            return carry

        lax.fori_loop(0, blocks, body, 0)

    receive(1)
    for copy in shared:
        copy.wait_recv()
    square = squares[0]
    for k in range(1, m):
        square = square + squares[k]
    square = jnp.broadcast_to(square[:1], (128, rows)).T
    inv_ref[...] = lax.rsqrt(square * (1.0 / model_width) + 1e-05)
    for load in loads:
        load.wait()
    project(t, True)
    project(origin_of(1, 0), False)
    project(origin_of(1, 1), False)
    for distance in range(2, m // 2 + 1):
        receive(distance)
        project(origin_of(distance, 0), False)
        if 2 * distance != m:
            project(origin_of(distance, 1), False)

    def prompt_rows(value):
        return value.reshape(n, chunk, value.shape[-1])[:, split:].reshape(
            n * lead, value.shape[-1]
        )

    limit = p_len + pick(me, lambda e: length_ref[e])
    scale = 1.0 / math.sqrt(HD)

    def heads(g, carry):
        cosine, sine = cos_ref[...], sin_ref[...]
        cosine_p, sine_p = prompt_rows(cosine), prompt_rows(sine)
        row_pos, col_pos = posr_ref[...], posc_ref[...]
        allowed = (col_pos <= row_pos) & (col_pos < limit)
        live = row_pos < limit
        for h in range(group // HD):
            at = slice(h * HD, (h + 1) * HD)
            far = pl.ds(pl.multiple_of(g * group + h * HD, HD), HD)
            q, k = qkv[g, :, at], qkv[per + g, :, at]
            v = qkv[2 * per + g, :, at].astype(bf16)
            q = (q * cosine + pltpu.roll(q, HD // 2, 1) * sine).astype(bf16)
            k = (k * cosine + pltpu.roll(k, HD // 2, 1) * sine).astype(bf16)
            scores = jnp.where(allowed, dot_nt(q, k) * scale, -1e30)
            peak = jnp.max(scores, axis=1, keepdims=True)
            weights = jnp.exp(scores - peak)
            probs = weights * (1.0 / jnp.sum(weights, axis=1, keepdims=True))
            low = probs.astype(bf16)
            out_ref[:, far] = jnp.where(live, dot_nn(low, v), 0.0).astype(bf16)
            upstream = jnp.where(live, cot_ref[:, far].astype(f32), 0.0).astype(bf16)
            grad_prob = dot_nt(upstream, v)
            delta = jnp.sum(probs * grad_prob, axis=1, keepdims=True)
            grad_score = probs * (grad_prob - delta)
            gq = dot_nn(prompt_rows(grad_score).astype(bf16), k) * scale
            gk = prompt_rows(dot_tn(grad_score.astype(bf16), q)) * scale
            gv = prompt_rows(dot_tn(low, upstream))
            gq = gq * cosine_p - pltpu.roll(gq, HD // 2, 1) * sine_p
            gk = gk * cosine_p - pltpu.roll(gk, HD // 2, 1) * sine_p
            grads[g, :, at] = gq.astype(bf16)
            grads[per + g, :, at] = gk.astype(bf16)
            grads[2 * per + g, :, at] = gv.astype(bf16)
        return carry

    lax.fori_loop(0, per, heads, 0)

    def prompts_of(z):
        return full[z, :, split:, :].astype(f32).reshape(n * lead, width)

    def back(z, dots):
        deep = pl.ds(pl.multiple_of(z * width, width), width)
        total = dot_nt(grads[0], w_ref[0, deep, :])
        for b in range(1, blocks):
            total = total + dot_nt(grads[b], w_ref[b, deep, :])
        total = total * gain_ref[z]
        acc[z] = total
        return dots + jnp.sum(total * prompts_of(z), axis=1, keepdims=True)

    dots = lax.fori_loop(0, m, back, jnp.zeros((n * lead, 1), f32))
    inv = prompt_rows(inv_ref[...])[:, :1]
    factor = inv * inv * inv * (dots * (1.0 / model_width))

    partial = {}
    for step in range(m):
        z = lax.rem(t + (2, 1, 3, 0)[step] if m == 4 else t + m - 1 - step, m)
        value = (inv * acc[z] - prompts_of(z) * factor).astype(bf16)
        part[z] = value.reshape(n, lead, width)
        if step < m - 1:
            for k in range(n):
                at = lax.rem(me + k, n)
                sems = (semg.at[0, step, k], semg.at[1, step, k])
                partial[step, k] = remote(
                    part.at[z, at], recvz.at[step, at], sems, (me, z), holds(at)
                )

    third = []
    for k in range(n):
        at = lax.rem(me + k, n)

        @pl.when(holds(at))
        def _():
            total = part[t, at].astype(f32)
            for step in range(m - 1):
                partial[step, k].wait_recv()
                total = total + recvz[step, at].astype(f32)
            if k == 0:
                recv1[me] = total.astype(bf16)
            else:
                send1[k] = total.astype(bf16)

        if k:
            sems = (sem3.at[0, k], sem3.at[1, k])
            third.append(remote(send1.at[k], recv1.at[me], sems, (at, t), holds(at)))

    @pl.when(holds(me))
    def _():
        for copy in third:
            copy.wait_recv()

    tasks = [task_at(s) for s in range(n)]
    fourth = []
    for k in range(n):
        peer = lax.rem(me + k, n)

        @pl.when(holds(me))
        def _():
            total = jnp.zeros((lead, width), f32)
            for s in range(n):
                hit = jnp.where(tasks[s] == peer, 1.0, 0.0)
                total = total + hit * recv1[s].astype(f32)
            if k == 0:
                recv2[me] = total.astype(bf16)
            else:
                send2[k] = total.astype(bf16)

        if k:
            sems = (sem4.at[0, k], sem4.at[1, k])
            fourth.append(remote(send2.at[k], recv2.at[me], sems, (peer, t), holds(me)))
    for k in range(1, n):
        pl.when(holds(lax.rem(me + n - k, n)))(fourth[k - 1].wait_recv)
    for at in range(n):
        if at * lead < p_len:
            grad_ref[at] = recv2[at].astype(f32)
        else:
            grad_ref[at] = jnp.zeros((lead, width), f32)
    for copy in first + second + list(hops.values()) + shared:
        copy.wait_send()
    for (_, k), copy in partial.items():
        pl.when(holds(lax.rem(me + k, n)))(copy.wait_send)
    for k in range(1, n):
        pl.when(holds(lax.rem(me + k, n)))(third[k - 1].wait_send)
        pl.when(holds(me))(fourth[k - 1].wait_send)


def fast_device(text, prompts, gain, w_query, w_key, w_value, cotangent, task_of, lengths, slot):
    n, m = lax.axis_size("dp"), lax.axis_size("tensor")
    f32, bf16 = jnp.float32, jnp.bfloat16
    seq, width = text.shape[1], text.shape[2]
    p_len = prompts.shape[1]
    ct = seq // n
    cp = ct // 2
    chunk = ct + cp
    rows = n * chunk
    heads = w_query.shape[1]

    def interleave(tail, lead):
        lead = jnp.pad(lead, ((0, n * cp - p_len), (0, 0)))
        parts = [tail.reshape(n, ct, -1), lead.reshape(n, cp, -1)]
        return jnp.concatenate(parts, axis=1)

    row = np.arange(rows, dtype=np.int32)
    j, i = row // chunk, row % chunk
    lead_pos = j * cp + i - ct
    lead_pos = np.where(lead_pos < p_len, lead_pos, PAD_POS)
    pos = np.where(i < ct, p_len + j * ct + i, lead_pos).astype(np.int32)
    half = HD // 2
    frequency = 10000.0 ** (-jnp.arange(half, dtype=f32) / half)
    angle = jnp.asarray(np.where(pos < PAD_POS, pos, 0)).astype(f32)[:, None] * frequency[None, :]
    cosine = jnp.concatenate([jnp.cos(angle)] * 2, axis=1)
    sine = jnp.concatenate([-jnp.sin(angle), jnp.sin(angle)], axis=1)
    cot = interleave(cotangent[0, p_len:], cotangent[0, :p_len]).reshape(rows, heads)
    group = 2 * HD if heads % (2 * HD) == 0 else HD
    blocks = 3 * (heads // group)
    smem = pl.BlockSpec(memory_space=pltpu.SMEM)
    vmem = pl.BlockSpec(memory_space=pltpu.VMEM)
    hbm = pl.BlockSpec(memory_space=pl.ANY)
    dma = pltpu.SemaphoreType.DMA
    out, collected = pl.pallas_call(
        functools.partial(step_kernel, p_len),
        out_shape=(
            jax.ShapeDtypeStruct((rows, heads), bf16),
            jax.ShapeDtypeStruct((n, cp, width), f32),
        ),
        in_specs=[smem] * 3 + [vmem] * 7 + [hbm] * 3,
        out_specs=(vmem, vmem),
        scratch_shapes=[
            pltpu.VMEM((blocks, m * width, group), bf16),
            pltpu.VMEM((n, chunk, width), bf16),
            pltpu.VMEM((n, chunk, width), bf16),
            pltpu.VMEM((m, n, chunk, width), bf16),
            pltpu.VMEM((m, 8, rows), f32),
            pltpu.VMEM((blocks, rows, group), f32),
            pltpu.VMEM((blocks, n * cp, group), bf16),
            pltpu.VMEM((rows, 128), f32),
            pltpu.VMEM((m, n * cp, width), f32),
            pltpu.VMEM((m, n, cp, width), bf16),
            pltpu.VMEM((m - 1, n, cp, width), bf16),
            pltpu.VMEM((n, cp, width), bf16),
            pltpu.VMEM((n, cp, width), bf16),
            pltpu.VMEM((n, cp, width), bf16),
            pltpu.VMEM((n, cp, width), bf16),
            dma((blocks,)),
            dma((2, n)),
            dma((2, n)),
            dma((2, 2, m // 2 + 1, n)),
            dma((2, m)),
            dma((2, m, n)),
            dma((2, n)),
            dma((2, n)),
        ],
        compiler_params=pltpu.CompilerParams(
            collective_id=0, has_side_effects=True, vmem_limit_bytes=63 * 2**20
        ),
    )(
        slot, task_of, lengths, interleave(text[0], prompts[0]), gain.reshape(m, 1, width),
        cosine, sine, jnp.asarray(pos[:, None]), jnp.asarray(pos[None, :]), cot, w_query, w_key, w_value,
    )
    prompt_grad = collected.reshape(n * cp, width)[:p_len][None]
    out = out.reshape(n, chunk, heads)
    lead = out[:, ct:].reshape(n * cp, heads)[:p_len]
    attn_out = jnp.concatenate([lead, out[:, :ct].reshape(seq, heads)], axis=0)[None]
    return (attn_out, prompt_grad)


def choose(text, prompts, *rest):
    n, m = lax.axis_size("dp"), lax.axis_size("tensor")
    seq, p_len = text.shape[1], prompts.shape[1]
    fits = (
        text.shape[0] == 1
        and prompts.shape[0] == 1
        and m >= 3
        and n >= 2
        and seq % (32 * n) == 0
        and p_len <= seq // 2
        and text.shape[2] % 128 == 0
    )
    return (fast_device if fits else on_device)(text, prompts, *rest)


def solution(mesh):
    in_specs = (
        P("dp", None, "tensor"),
        P("dp", None, "tensor"),
        P(),
        P(None, "tensor"),
        P(None, "tensor"),
        P(None, "tensor"),
        P("dp", None, "tensor"),
        P(),
        P(),
        P(),
    )
    out_specs = (P("dp", None, "tensor"), P("dp", None, "tensor"))
    return jax.shard_map(
        choose, mesh=mesh, in_specs=in_specs, out_specs=out_specs, check_vma=False
    )
```

profile of v0, /device:TPU:11, one launch (start us, length us, event | category | flops | bytes accessed | tf_op | source)
XLA Modules:
  0.0 151.5 jit_solution(13991188341100407334)
XLA Ops:
  0.6 0.0 copy-start.2
  0.7 0.9 slice_bitcast_fusion
  1.6 0.0 copy-start
  1.6 1.0 pad.8
  2.7 1.1 slice.18
  3.8 0.9 pad_maximum_fusion.1
  4.6 0.0 copy-done.2
  4.6 0.8 fusion
  5.4 0.9 pad_maximum_fusion.2
  6.3 0.0 copy-done
  6.3 1.0 pad_maximum_fusion.inp_ref
  7.3 140.9 %shard_map.140 = (bf16[384,768]{1,0:T(8,128)(2,1)}, f32[8,16,1280]{2,1,0:T(8,128)}) custom-call(s32[8]{0:T(128)} %slot_ref.1, s32[8]{0:T(128)} %task_ref.1, s32[8]{0:T(128)} %length_ref.1, bf16[8,48,1280]{2,1,0:T(8,128)(2,1)} %pad_maximum_fusion.inp_ref, f32[4,1,1280]{2,1,0:T(1,128)} %bitcast.26, f32[384,128]{1,0:T(8,128)} %get-tuple-element.9.cos_ref, ...), custom_call_target="tpu_custom_call" | custom-call | tf_op jit(solution)/shard_map/pallas_call | solution.py:537
  148.2 0.0 copy-start.1
  148.2 1.1 slice.27
  149.4 1.1 broadcast_in_dim.9
  150.5 0.0 copy-done.1
  150.6 0.9 maximum_bitcast_fusion
  (5 shorter events, 0.1 us)
Async XLA Ops:
  0.6 4.0 %copy-start.2 = (f32[384]{0:T(512)S(1)}, f32[384]{0:T(512)}, u32[]{:S(2)}) copy-start(f32[384]{0:T(512)} %constant.24) | copy-start | bytes 4612
  1.6 4.7 %copy-start = (bf16[1,256,1280]{2,1,0:T(8,128)(2,1)S(1)}, bf16[1,256,1280]{2,1,0:T(8,128)(2,1)}, u32[]{:S(2)}) copy-start(bf16[1,256,1280]{2,1,0:T(8,128)(2,1)} %param.13) | copy-start | bytes 1966084
  148.2 2.3 %copy-start.1 = (bf16[384,768]{1,0:T(8,128)(2,1)S(1)}, bf16[384,768]{1,0:T(8,128)(2,1)}, u32[]{:S(2)}) copy-start(bf16[384,768]{1,0:T(8,128)(2,1)} %get-tuple-element.4) | copy-start | bytes 1769476
where the time goes:
time: 152 us; the launch traced here: 151 us
  Pallas kernels  141 us (93%)
  local copies, waits for them, and re-layouts  5.43 us (4%)
  other arithmetic  4.47 us (3%)
    pallas_call x1, Pallas kernels, fast_device(): pl.pallas_call(functools.partial(step_kernel, p_len), out_shape=(jax.Shap...  141 us

commit v1 on v0

v1 whole, which is shorter than its diff:
```python
import functools
import math

import jax
import jax.numpy as jnp
import numpy as np
from jax import lax
from jax.experimental import pallas as pl
from jax.experimental.pallas import tpu as pltpu
from jax.sharding import PartitionSpec as P

HD = 128


def rope_tables(row_count):
    half_dim = HD // 2
    frequency = 10000.0 ** (-jnp.arange(half_dim, dtype=jnp.float32) / half_dim)
    angle_table = jnp.arange(row_count, dtype=jnp.float32)[:, None] * frequency[None, :]
    return (jnp.cos(angle_table), jnp.sin(angle_table))


def rotate(vectors, cosine_table, sine_table):
    half_dim = vectors.shape[-1] // 2
    first_half = vectors[..., :half_dim]
    second_half = vectors[..., half_dim:]
    cosine_b = cosine_table[:, None, :]
    sine_b = sine_table[:, None, :]
    return jnp.concatenate(
        [
            first_half * cosine_b - second_half * sine_b,
            second_half * cosine_b + first_half * sine_b,
        ],
        axis=-1,
    )


def unrotate(vectors, cosine_table, sine_table):
    half_dim = vectors.shape[-1] // 2
    first_half = vectors[..., :half_dim]
    second_half = vectors[..., half_dim:]
    cosine_b = cosine_table[:, None, :]
    sine_b = sine_table[:, None, :]
    return jnp.concatenate(
        [
            first_half * cosine_b + second_half * sine_b,
            second_half * cosine_b - first_half * sine_b,
        ],
        axis=-1,
    )


def transpose_product(grad_low, matrix):
    return lax.dot_general(
        grad_low, matrix, (((1,), (1,)), ((), ())), preferred_element_type=jnp.float32
    )


def attention_window(full_rows, gain, w_query, w_key, w_value, cotangent, valid_rows, prompt_len):
    batch_size, row_count, model_width = full_rows.shape
    head_count = w_query.shape[1] // HD
    wide_rows = full_rows.astype(jnp.float32)
    inv_rms = lax.rsqrt(jnp.mean(wide_rows * wide_rows, axis=-1) + 1e-05)
    normed = (
        (wide_rows * inv_rms[..., None] * gain)
        .astype(jnp.bfloat16)
        .reshape(batch_size * row_count, model_width)
    )
    cosine_table, sine_table = rope_tables(row_count)

    def project(matrix):
        return jnp.dot(normed, matrix, preferred_element_type=jnp.float32).reshape(
            batch_size, row_count, head_count, HD
        )

    queries = rotate(project(w_query), cosine_table, sine_table).astype(jnp.bfloat16)
    key_rows = rotate(project(w_key), cosine_table, sine_table).astype(jnp.bfloat16)
    value_rows = project(w_value).astype(jnp.bfloat16)
    score_scale = 1.0 / math.sqrt(HD)
    scores = (
        jnp.einsum("erhd,ekhd->ehrk", queries, key_rows, preferred_element_type=jnp.float32)
        * score_scale
    )
    rows_at = jnp.arange(row_count, dtype=jnp.int32)
    row_limit = prompt_len + valid_rows
    allowed = (rows_at[None, None, :] <= rows_at[None, :, None]) & (
        rows_at[None, None, :] < row_limit[:, None, None]
    )
    allowed = allowed[:, None]
    scores = jnp.where(allowed, scores, -1e30)
    row_peak = jnp.max(scores, axis=-1, keepdims=True)
    weights = jnp.where(allowed, jnp.exp(scores - row_peak), 0.0)
    probability = weights / jnp.sum(weights, axis=-1, keepdims=True)
    probs_low = probability.astype(jnp.bfloat16)
    live_rows = rows_at[None, :] < row_limit[:, None]
    mixed_rows = jnp.einsum(
        "ehrk,ekhd->erhd", probs_low, value_rows, preferred_element_type=jnp.float32
    )
    mixed_rows = jnp.where(live_rows[:, :, None, None], mixed_rows, 0.0)
    output = mixed_rows.reshape(batch_size, row_count, head_count * HD).astype(jnp.bfloat16)
    upstream = jnp.where(
        live_rows[:, :, None, None], cotangent.reshape(batch_size, row_count, head_count, HD), 0.0
    )
    grad_prob = jnp.einsum(
        "erhd,ekhd->ehrk", upstream, value_rows, preferred_element_type=jnp.float32
    )
    row_delta = jnp.sum(probability * grad_prob, axis=-1, keepdims=True)
    grad_score = (probability * (grad_prob - row_delta)).astype(jnp.bfloat16)
    grad_query = (
        jnp.einsum(
            "ehrk,ekhd->erhd",
            grad_score[:, :, :prompt_len, :],
            key_rows,
            preferred_element_type=jnp.float32,
        )
        * score_scale
    )
    grad_key = (
        jnp.einsum(
            "ehrk,erhd->ekhd",
            grad_score[:, :, :, :prompt_len],
            queries,
            preferred_element_type=jnp.float32,
        )
        * score_scale
    )
    grad_value = jnp.einsum(
        "ehrk,erhd->ekhd",
        probs_low[:, :, :, :prompt_len],
        upstream,
        preferred_element_type=jnp.float32,
    )
    cosine_lead = cosine_table[:prompt_len]
    sine_lead = sine_table[:prompt_len]
    flat_rows = batch_size * prompt_len
    grad_query = (
        unrotate(grad_query, cosine_lead, sine_lead)
        .astype(jnp.bfloat16)
        .reshape(flat_rows, head_count * HD)
    )
    grad_key = (
        unrotate(grad_key, cosine_lead, sine_lead)
        .astype(jnp.bfloat16)
        .reshape(flat_rows, head_count * HD)
    )
    grad_value = grad_value.astype(jnp.bfloat16).reshape(flat_rows, head_count * HD)
    grad_normed = (
        transpose_product(grad_query, w_query)
        + transpose_product(grad_key, w_key)
        + transpose_product(grad_value, w_value)
    )
    grad_normed = grad_normed.reshape(batch_size, prompt_len, model_width) * gain
    prompt_rows = wide_rows[:, :prompt_len]
    prompt_inv = inv_rms[:, :prompt_len, None]
    grad_rows = prompt_inv * grad_normed - prompt_rows * prompt_inv**3 * jnp.mean(
        grad_normed * prompt_rows, axis=-1, keepdims=True
    )
    return (output, grad_rows)


def on_device(text, prompts, gain, w_query, w_key, w_value, cotangent, task_of, lengths, slot):
    dp_count = lax.axis_size("dp")
    my_index = lax.axis_index("dp")
    ex_dev = text.shape[0]
    task_dev = prompts.shape[0]
    prompt_len = prompts.shape[1]
    example_count = slot.shape[0]
    task_count = task_dev * dp_count
    places = jnp.arange(example_count, dtype=jnp.int32)
    matching = slot[None, :] == places[:, None]
    task_slot = jnp.sum(jnp.where(matching, task_of[None, :], 0), axis=1)
    length_slot = jnp.sum(jnp.where(matching, lengths[None, :], 0), axis=1)
    first_place = my_index * ex_dev
    my_lengths = lax.dynamic_slice_in_dim(length_slot, first_place, ex_dev)
    task_ids = jnp.arange(task_count, dtype=jnp.int32)
    spread_text, spread_prompts = (
        lax.all_to_all(text, "dp", split_axis=2, concat_axis=0, tiled=True),
        lax.all_to_all(prompts, "dp", split_axis=2, concat_axis=0, tiled=True),
    )
    taking = matching.astype(jnp.bfloat16)
    placed_text = jnp.einsum(
        "se,erc->src", taking, spread_text, preferred_element_type=jnp.bfloat16
    )
    choosing = (task_slot[:, None] == task_ids[None, :]).astype(jnp.bfloat16)
    placed_prompts = jnp.einsum(
        "st,tpc->spc", choosing, spread_prompts, preferred_element_type=jnp.bfloat16
    )
    placed = jnp.concatenate([placed_prompts, placed_text], axis=1)
    placed = placed.reshape(dp_count, ex_dev, placed.shape[1], placed.shape[2])
    local_rows = lax.all_to_all(placed, "dp", split_axis=0, concat_axis=3, tiled=True)[0]
    full_rows = lax.all_gather(local_rows, "tensor", axis=2, tiled=True)
    output, grad_part = attention_window(
        full_rows, gain, w_query, w_key, w_value, cotangent, my_lengths, prompt_len
    )
    grad_share = lax.psum_scatter(grad_part, "tensor", scatter_dimension=2, tiled=True)
    spread_grads = lax.all_to_all(grad_share, "dp", split_axis=2, concat_axis=0, tiled=True)
    collecting = (task_ids[:, None] == task_slot[None, :]).astype(jnp.float32)
    per_task = jnp.einsum("ts,spc->tpc", collecting, spread_grads, precision=lax.Precision.HIGHEST)
    prompt_grad = lax.all_to_all(per_task, "dp", split_axis=0, concat_axis=2, tiled=True)
    return (output, prompt_grad)


MESH = pl.DeviceIdType.MESH
PAD_POS = 1 << 20
TILE = 8


def dot_nn(a, b):
    return jnp.dot(a, b, preferred_element_type=jnp.float32)


def dot_nt(a, b):
    return lax.dot_general(a, b, (((1,), (1,)), ((), ())), preferred_element_type=jnp.float32)


def dot_tn(a, b):
    return lax.dot_general(a, b, (((0,), (0,)), ((), ())), preferred_element_type=jnp.float32)


def partner(me, k):
    bit, peer = 1, me
    while bit <= k:
        if k & bit:
            peer = peer + bit - 2 * bit * lax.rem(me // bit, 2)
        bit *= 2
    return peer


def origin_table(m):
    table = []
    for t in range(m):
        others = [z for z in range(m) if z != t]
        others.sort(key=lambda z: (abs(z - t), (z < t) == (2 * t < m)))
        table.append(others)
    return table


def step_kernel(
    p_len, slot_ref, task_ref, length_ref, text_ref, prompts_ref, gain_ref, cos_ref, sin_ref,
    cot_ref, wq_hbm, wk_hbm, wv_hbm, out_ref, grad_ref,
    w_ref, pbuf, precv, psend, fullp, tz, stage, tsend, fullt, squares, qkv, grads, inv_ref, cot_pad,
    part, pin, send4, gout,
    semw, sem_t, sem_p, sem_c, sem_s, semz_own, semz_fwd, semz_in, semq, semg, semg_in, sem4,
):
    n, m = lax.axis_size("dp"), lax.axis_size("tensor")
    me, t = lax.axis_index("dp"), lax.axis_index("tensor")
    f32, bf16 = jnp.float32, jnp.bfloat16
    tu, _, _, width = text_ref.shape
    blocks, model_width, group = w_ref.shape
    per = blocks // 3
    pt = -(-p_len // TILE)
    pu = -(-pt // n)
    lead = pt * TILE
    seq = tu * n * TILE
    rows = lead + seq
    counts = [min(n, pt - v * n) for v in range(pu)]
    peers = [partner(me, k) for k in range(n)]
    table = origin_table(m)

    def pick(place, values):
        total = jnp.int32(0)
        for e in range(n):
            total = jnp.maximum(total, jnp.where(slot_ref[e] == place, values(e), 0))
        return total

    def by_place(values):
        total = jnp.int32(0)
        for z in range(m):
            total = total + jnp.where(t == z, values[z], 0)
        return total

    origins = [by_place([table[z][i] for z in range(m)]) for i in range(m - 1)]

    def describe(src, dst, send, recv, device):
        return pltpu.make_async_remote_copy(
            src_ref=src,
            dst_ref=dst,
            send_sem=send,
            recv_sem=recv,
            device_id=device,
            device_id_type=MESH,
        )

    waits = []

    def remote(src, dst, send, recv, device, needed=None):
        copy = describe(src, dst, send, recv, device)
        if needed is None:
            copy.start()
        else:
            pl.when(needed)(copy.start)
        waits.append((copy, needed))
        return copy

    loads = []
    for i, hbm in enumerate((wq_hbm, wk_hbm, wv_hbm)):
        for g in range(per):
            at = i * per + g
            load = pltpu.make_async_copy(
                hbm.at[:, g * group : (g + 1) * group], w_ref.at[at], semw.at[at]
            )
            load.start()
            loads.append(load)

    barrier = pltpu.get_barrier_semaphore()
    for z in range(m):
        for k in range(n):
            far = lax.rem(t + z, m)
            if z or k:
                pl.semaphore_signal(
                    barrier, inc=1, device_id=(peers[k], far), device_id_type=MESH
                )

    whole = p_len // TILE
    pbuf[:whole] = prompts_ref[: whole * TILE].reshape(whole, TILE, width)
    if p_len % TILE:
        rest = prompts_ref[whole * TILE : p_len].astype(f32)
        fill = jnp.zeros((TILE - p_len % TILE, width), f32)
        pbuf[whole] = jnp.concatenate([rest, fill], axis=0).astype(bf16)
    if pu * n > pt:
        pbuf[pt:] = jnp.zeros((pu * n - pt, TILE, width), bf16)
    cot_pad[:lead] = cot_ref[:lead]
    cot_pad[lead:] = cot_ref[p_len:].astype(f32).astype(bf16)
    pl.semaphore_wait(barrier, n * m - 1)

    spread_0, spread_t, spread_p = [], [], []
    for k in range(1, n):
        spread_0.append(
            remote(
                text_ref.at[0, peers[k]], tz.at[t, 0, me],
                sem_t.at[0, 0, k], sem_t.at[1, 0, k], (peers[k], t),
            )
        )
    for k in range(1, n):
        if tu > 1:
            spread_t.append(
                remote(
                    text_ref.at[1:, peers[k]], tz.at[t, 1:, me],
                    sem_t.at[0, 1, k], sem_t.at[1, 1, k], (peers[k], t),
                )
            )
    for k in range(1, n):
        for v in range(pu):
            spread_p.append(
                remote(
                    pbuf.at[v * n + peers[k]], precv.at[v, me],
                    sem_p.at[0, v, k], sem_p.at[1, v, k], (peers[k], t),
                )
            )
    for u in range(tu):
        tz[t, u, me] = text_ref[u, me]
    for v in range(pu):
        precv[v, me] = pbuf[v * n + me]

    ways = [(t < m - 1, lax.rem(t + 1, m)), (t > 0, lax.rem(t + m - 1, m))]

    def text_unit(z, g):
        return tz.at[z, g]

    def prompt_unit(z, v):
        return fullp.at[z, v, : counts[v]]

    units = [(text_unit, g) for g in range(tu)] + [(prompt_unit, v) for v in range(pu)]

    def pass_own(i):
        ref = units[i][0](t, units[i][1])
        for w, (needed, far) in enumerate(ways):
            remote(ref, ref, semz_own.at[w, i], semz_in.at[t, i], (me, far), needed)

    for copy in spread_0:
        copy.wait_recv()
    pass_own(0)
    for copy in spread_t:
        copy.wait_recv()
    for g in range(1, tu):
        pass_own(g)

    sources = [pick(peers[k], lambda e: e) for k in range(n)]
    tasks_of = [pick(peers[k], lambda e: task_ref[e]) for k in range(n)]

    for copy in spread_p:
        copy.wait_recv()
    collect_p = []
    for k in range(1, n):
        for v in range(pu):
            psend[k, v] = precv[v, tasks_of[k]]
        collect_p.append(
            remote(
                psend.at[k], fullp.at[t, :, me], sem_c.at[0, k], sem_c.at[1, k], (peers[k], t)
            )
        )
    for v in range(pu):
        fullp[t, v, me] = precv[v, tasks_of[0]]
    collected = {}

    def collect(i, z, lo, hi):
        for u in range(lo, hi):
            stage[u - lo] = tz[z, u]
        for k in range(1, n):
            for u in range(lo, hi):
                tsend[i, k, u] = stage[u - lo, sources[k]]
            collected[i, lo, k] = remote(
                tsend.at[i, k, lo:hi], fullt.at[z, lo:hi, me],
                sem_s.at[0, i, lo, k], sem_s.at[1, i, lo, k], (peers[k], t),
            )
        for u in range(lo, hi):
            fullt[z, u, me] = stage[u - lo, sources[0]]

    def finish(i):
        for key, copy in collected.items():
            if key[0] == i:
                copy.wait_recv()

    collect(m - 1, t, 0, tu)
    for copy in collect_p:
        copy.wait_recv()
    for v in range(pu):
        pass_own(tu + v)
    finish(m - 1)

    def whole_rows(z):
        prompt = fullp[z].reshape(pu * n * TILE, width)[:lead]
        return jnp.concatenate([prompt, fullt[z].reshape(seq, width)], axis=0)

    own = whole_rows(t).astype(f32)
    square = jnp.broadcast_to(jnp.sum(own * own, axis=1, keepdims=True), (rows, 128))
    padded = squares.shape[2]
    square = jnp.concatenate([square, jnp.zeros((padded - rows, 128), f32)], axis=0)
    squares[0] = square.T[:8]
    shared = []
    for k in range(1, m):
        shared.append(
            remote(
                squares.at[0], squares.at[k], semq.at[0, k], semq.at[1, k],
                (me, lax.rem(t + k, m)),
            )
        )

    def project(z, fresh):
        wide = whole_rows(z).astype(f32)
        normed = (wide * inv_ref[:, :1] * gain_ref[z]).astype(bf16)
        deep = pl.ds(pl.multiple_of(z * width, width), width)

        def body(b, carry):
            product = dot_nn(normed, w_ref[b, deep, :])
            qkv[b] = product if fresh else qkv[b] + product
            return carry

        lax.fori_loop(0, blocks, body, 0)

    def receive(i):
        z = origins[i]
        left = z < t
        needed = (left & (t < m - 1)) | (jnp.logical_not(left) & (t > 0))
        far = jnp.where(needed, jnp.where(left, t + 1, t - 1), z)
        step = 1 if i == m - 2 else max(1, tu // 2)
        for j, (unit, g) in enumerate(units):
            ref = unit(z, g)
            describe(ref, ref, semz_fwd.at[i, j], semz_in.at[z, j], (me, far)).wait_recv()
            remote(ref, ref, semz_fwd.at[i, j], semz_in.at[z, j], (me, far), needed)
            if j < tu and (j + 1) % step == 0:
                collect(i, z, j + 1 - step, j + 1)
        finish(i)

    receive(0)
    for copy in shared:
        copy.wait_recv()
    square = squares[0]
    for k in range(1, m):
        square = square + squares[k]
    square = jnp.broadcast_to(square[:1], (128, padded)).T[:rows]
    inv_ref[...] = lax.rsqrt(square * (1.0 / model_width) + 1e-05)
    for load in loads:
        load.wait()
    project(t, True)
    project(origins[0], False)
    for i in range(1, m - 1):
        receive(i)
        project(origins[i], False)

    limit = p_len + pick(me, lambda e: length_ref[e])
    scale = 1.0 / math.sqrt(HD)

    def positions(shape, axis):
        at = lax.broadcasted_iota(jnp.int32, shape, axis)
        return jnp.where(at < lead, jnp.where(at < p_len, at, PAD_POS), at - (lead - p_len))

    def heads(g, dots):
        cosine, sine = cos_ref[...], sin_ref[...]
        cosine_p, sine_p = cosine[:lead], sine[:lead]
        row_pos = positions((rows, 1), 0)
        col_pos = positions((1, rows), 1)
        allowed = (col_pos <= row_pos) & (col_pos < limit)
        live = row_pos < limit
        edge = min(rows, -(-lead // 128) * 128)
        for h in range(group // HD):
            at = slice(h * HD, (h + 1) * HD)
            far = pl.ds(pl.multiple_of(g * group + h * HD, HD), HD)
            q_raw, k_raw, v_raw = qkv[g, :, at], qkv[per + g, :, at], qkv[2 * per + g, :, at]
            v = v_raw.astype(bf16)
            q = (q_raw * cosine + pltpu.roll(q_raw, HD // 2, 1) * sine).astype(bf16)
            k = (k_raw * cosine + pltpu.roll(k_raw, HD // 2, 1) * sine).astype(bf16)
            scores = jnp.where(allowed, dot_nt(q, k) * scale, -1e30)
            peak = jnp.max(scores, axis=1, keepdims=True)
            weights = jnp.exp(scores - peak)
            probs = weights * (1.0 / jnp.sum(weights, axis=1, keepdims=True))
            low = probs.astype(bf16)
            out_ref[:, far] = jnp.where(live, dot_nn(low, v), 0.0).astype(bf16)
            upstream = jnp.where(live, cot_pad[:, far].astype(f32), 0.0).astype(bf16)
            grad_prob = dot_nt(upstream, v)
            delta = jnp.sum(probs * grad_prob, axis=1, keepdims=True)
            grad_score = (probs * (grad_prob - delta)).astype(bf16)
            gq = dot_nn(grad_score[:lead, :edge], k[:edge]) * scale
            gk = dot_tn(grad_score[:, :edge], q)[:lead] * scale
            gv = dot_tn(low[:, :edge], upstream)[:lead]
            gq = (gq * cosine_p - pltpu.roll(gq, HD // 2, 1) * sine_p).astype(bf16)
            gk = (gk * cosine_p - pltpu.roll(gk, HD // 2, 1) * sine_p).astype(bf16)
            gv = gv.astype(bf16)
            grads[g, :, at] = gq
            grads[per + g, :, at] = gk
            grads[2 * per + g, :, at] = gv
            along = gq.astype(f32) * q_raw[:lead] + gk.astype(f32) * k_raw[:lead]
            along = along + gv.astype(f32) * v_raw[:lead]
            dots = dots + jnp.sum(along, axis=1, keepdims=True)
        return dots

    dots = lax.fori_loop(0, per, heads, jnp.zeros((lead, 1), f32))
    inv = inv_ref[:lead, :1]
    factor = inv * inv * (dots * (1.0 / model_width))

    def holds(v, at):
        return None if counts[v] == n else v * n + at < pt

    def when(needed, act):
        if needed is None:
            act()
        else:
            pl.when(needed)(act)

    for i in range(m):
        z = origins[m - 2 - i] if i < m - 1 else t
        deep = pl.ds(pl.multiple_of(z * width, width), width)
        total = dot_nt(grads[0], w_ref[0, deep, :])
        for b in range(1, blocks):
            total = total + dot_nt(grads[b], w_ref[b, deep, :])
        prompt = fullp[z].reshape(pu * n * TILE, width)[:lead].astype(f32)
        value = inv * (total * gain_ref[z]) - prompt * factor
        part[i, :pt] = value.astype(bf16).reshape(pt, TILE, width)
        for k in range(n):
            for v in range(pu):
                if i == m - 1 and k == 0:
                    continue
                remote(
                    part.at[i, v * n + peers[k]], pin.at[v, me, t],
                    semg.at[i, v, k], semg_in.at[v, k, t], (peers[k], z), holds(v, peers[k]),
                )
        if i == m - 1:
            for v in range(pu):

                def keep(v=v):
                    pin[v, me, t] = part[m - 1, v * n + me]

                when(holds(v, me), keep)

    tasks = [pick(s, lambda e: task_ref[e]) for s in range(n)]
    fourth = {}
    for v in range(pu):

        def gather(v=v):
            for k in range(n):
                for z in range(m):
                    spot = lax.rem(t + z, m)
                    if k or z:
                        describe(
                            pin.at[v, peers[k], spot], pin.at[v, peers[k], spot],
                            semg.at[0, v, k], semg_in.at[v, k, spot], (peers[k], spot),
                        ).wait_recv()
            for s in range(n):
                total = pin[v, s, 0].astype(f32)
                for z in range(1, m):
                    total = total + pin[v, s, z].astype(f32)
                for k in range(n):
                    hit = jnp.where(tasks[s] == peers[k], total, 0.0)
                    sums[k] = hit if s == 0 else sums[k] + hit
            for k in range(n):
                if k == 0:
                    gout[v, me] = sums[k].astype(bf16)
                else:
                    send4[v, k] = sums[k].astype(bf16)

        sums = [None] * n
        when(holds(v, me), gather)
        for k in range(1, n):
            fourth[v, k] = remote(
                send4.at[v, k], gout.at[v, me], sem4.at[0, v, k], sem4.at[1, v, k],
                (peers[k], t), holds(v, me),
            )
    for v in range(pu):
        for k in range(1, n):
            when(holds(v, peers[k]), fourth[v, k].wait_recv)
        grad_ref[v * n : v * n + counts[v]] = gout[v, : counts[v]]
    for copy, needed in waits:
        when(needed, copy.wait_send)


def fast_device(text, prompts, gain, w_query, w_key, w_value, cotangent, task_of, lengths, slot):
    n, m = lax.axis_size("dp"), lax.axis_size("tensor")
    f32, bf16 = jnp.float32, jnp.bfloat16
    seq, width = text.shape[1], text.shape[2]
    p_len = prompts.shape[1]
    heads = w_query.shape[1]
    tu = seq // (TILE * n)
    pt = -(-p_len // TILE)
    pu = -(-pt // n)
    lead = pt * TILE
    rows = lead + seq
    row = np.arange(rows)
    pos = np.where(row < lead, np.where(row < p_len, row, 0), row - (lead - p_len))
    half = HD // 2
    frequency = 10000.0 ** (-jnp.arange(half, dtype=f32) / half)
    angle = jnp.asarray(pos.astype(np.int32)).astype(f32)[:, None] * frequency[None, :]
    cosine = jnp.concatenate([jnp.cos(angle)] * 2, axis=1)
    sine = jnp.concatenate([-jnp.sin(angle), jnp.sin(angle)], axis=1)
    group = 2 * HD if heads % (2 * HD) == 0 else HD
    blocks = 3 * (heads // group)
    units = tu + pu
    smem = pl.BlockSpec(memory_space=pltpu.SMEM)
    vmem = pl.BlockSpec(memory_space=pltpu.VMEM)
    hbm = pl.BlockSpec(memory_space=pl.ANY)
    dma = pltpu.SemaphoreType.DMA
    out, collected = pl.pallas_call(
        functools.partial(step_kernel, p_len),
        out_shape=(
            jax.ShapeDtypeStruct((rows, heads), bf16),
            jax.ShapeDtypeStruct((pt, TILE, width), bf16),
        ),
        in_specs=[smem] * 3 + [vmem] * 6 + [hbm] * 3,
        out_specs=(vmem, vmem),
        scratch_shapes=[
            pltpu.VMEM((blocks, m * width, group), bf16),
            pltpu.VMEM((pu * n, TILE, width), bf16),
            pltpu.VMEM((pu, n, TILE, width), bf16),
            pltpu.VMEM((n, pu, TILE, width), bf16),
            pltpu.VMEM((m, pu, n, TILE, width), bf16),
            pltpu.VMEM((m, tu, n, TILE, width), bf16),
            pltpu.VMEM((tu, n, TILE, width), bf16),
            pltpu.VMEM((m, n, tu, TILE, width), bf16),
            pltpu.VMEM((m, tu, n, TILE, width), bf16),
            pltpu.VMEM((m, 8, -(-rows // 128) * 128), f32),
            pltpu.VMEM((blocks, rows, group), f32),
            pltpu.VMEM((blocks, lead, group), bf16),
            pltpu.VMEM((rows, 128), f32),
            pltpu.VMEM((rows, heads), bf16),
            pltpu.VMEM((m, pu * n, TILE, width), bf16),
            pltpu.VMEM((pu, n, m, TILE, width), bf16),
            pltpu.VMEM((pu, n, TILE, width), bf16),
            pltpu.VMEM((pu, n, TILE, width), bf16),
            dma((blocks,)),
            dma((2, 2, n)),
            dma((2, pu, n)),
            dma((2, n)),
            dma((2, m, tu, n)),
            dma((2, units)),
            dma((m, units)),
            dma((m, units)),
            dma((2, m)),
            dma((m, pu, n)),
            dma((pu, n, m)),
            dma((2, pu, n)),
        ],
        compiler_params=pltpu.CompilerParams(
            collective_id=0, has_side_effects=True, vmem_limit_bytes=63 * 2**20
        ),
    )(
        slot, task_of, lengths, text.reshape(tu, n, TILE, width), prompts[0],
        gain.reshape(m, 1, width), cosine, sine, cotangent[0], w_query, w_key, w_value,
    )
    prompt_grad = collected.reshape(lead, width)[:p_len].astype(f32)[None]
    attn_out = jnp.concatenate([out[:p_len], out[lead:]], axis=0)[None]
    return (attn_out, prompt_grad)


def choose(text, prompts, *rest):
    n, m = lax.axis_size("dp"), lax.axis_size("tensor")
    seq, p_len = text.shape[1], prompts.shape[1]
    fits = (
        text.shape[0] == 1
        and prompts.shape[0] == 1
        and m >= 2
        and n >= 2
        and n & (n - 1) == 0
        and n <= 8
        and seq % (TILE * n) == 0
        and text.shape[2] % 128 == 0
    )
    return (fast_device if fits else on_device)(text, prompts, *rest)


def solution(mesh):
    in_specs = (
        P("dp", None, "tensor"),
        P("dp", None, "tensor"),
        P(),
        P(None, "tensor"),
        P(None, "tensor"),
        P(None, "tensor"),
        P("dp", None, "tensor"),
        P(),
        P(),
        P(),
    )
    out_specs = (P("dp", None, "tensor"), P("dp", None, "tensor"))
    return jax.shard_map(
        choose, mesh=mesh, in_specs=in_specs, out_specs=out_specs, check_vma=False
    )
```

time: 152 us -> 136 us (0.89)
  Pallas kernels: 141 us -> 127 us
  local copies, waits for them, and re-layouts: 5.43 us -> 3.09 us
    pallas_call x1, Pallas kernels: 141 us -> 127 us  [fast_device(): pl.pallas_call(functools.partial(step_kernel, p_len), out_shape=(jax.Shap...]
    concatenate x2 -> x0, other arithmetic: 1.88 us -> none  [interleave(): return jnp.concatenate(parts, axis=1)]
where the time goes in v1:
time: 136 us; the launch traced here: 135 us
  Pallas kernels  127 us (93%)
  other arithmetic  4.21 us (3%)
  local copies, waits for them, and re-layouts  3.09 us (2%)
    pallas_call x1, Pallas kernels, fast_device(): pl.pallas_call(functools.partial(step_kernel, p_len), out_shape=(jax.Shap...  127 us

profile of v1, /device:TPU:11, one launch (start us, length us, event | category | flops | bytes accessed | tf_op | source)
XLA Modules:
  0.0 135.1 jit_solution(4058599107270189827)
XLA Ops:
  0.6 1.4 %fusion = (f32[360,64]{1,0:T(8,128)S(1)}, f32[360,64]{1,0:T(8,128)S(1)}, f32[360,64]{1,0:T(8,128)S(1)}) fusion(f32[64]{0:T(128)S(1)} %multiply_power_fusion, f32[360]{0:T(512)} %constant.11), kind=kLoop, calls=%fused_computation.6 | loop fusion | flops 46080 | bytes 278176 | tf_op jit(solution)/shard_map/neg | solution.py:622
  2.1 0.9 pad_maximum_fusion
  3.0 127.1 %shard_map.122 = (bf16[360,768]{1,0:T(8,128)(2,1)}, bf16[13,8,1280]{2,1,0:T(8,128)(2,1)}) custom-call(s32[8]{0:T(128)} %slot_ref.1, s32[8]{0:T(128)} %task_ref.1, s32[8]{0:T(128)} %length_ref.1, bf16[4,8,8,1280]{3,2,1,0:T(8,128)(2,1)} %bitcast.7, bf16[100,1280]{1,0:T(8,128)(2,1)} %bitcast.9, f32[4,1,1280]{2,1,0:T(1,128)} %bitcast.11, ...), custom_call_target="tpu_custom_call" | custom-call | tf_op jit(solution)/shard_map/pallas_call | solution.py:630
  130.1 0.9 slice.9
  131.0 1.0 slice.10
  132.0 0.9 maximum_bitcast_fusion
  132.9 1.0 slice_convert_fusion
  133.9 1.1 reshape.23
  (1 shorter events, 0.0 us)

commit v2 on v1

--- a/solution.py
+++ b/solution.py
@@ -235,11 +235,12 @@
 
 
 def step_kernel(
-    p_len, slot_ref, task_ref, length_ref, text_ref, prompts_ref, gain_ref, cos_ref, sin_ref,
-    cot_ref, wq_hbm, wk_hbm, wv_hbm, out_ref, grad_ref,
-    w_ref, pbuf, precv, psend, fullp, tz, stage, tsend, fullt, squares, qkv, grads, inv_ref, cot_pad,
+    p_len, slots, slot_ref, task_ref, length_ref, text_hbm, prompts_hbm, gain_hbm, cos_hbm, sin_hbm,
+    cot_hbm, wq_hbm, wk_hbm, wv_hbm, out_ref, grad_ref,
+    w_ref, text_ref, prompts_ref, gain_ref, cos_ref, sin_ref, cot_ref,
+    pbuf, precv, psend, fullp, trecv, tz, stage, tsend, fullt, squares, qkv, grads, inv_ref, cot_pad,
     part, pin, send4, gout,
-    semw, sem_t, sem_p, sem_c, sem_s, semz_own, semz_fwd, semz_in, semq, semg, semg_in, sem4,
+    semw, semi, sem_t, sem_p, sem_c, sem_s, semz_own, semz_fwd, semz_in, semq, semg, semg_in, sem4,
 ):
     n, m = lax.axis_size("dp"), lax.axis_size("tensor")
     me, t = lax.axis_index("dp"), lax.axis_index("tensor")
@@ -255,6 +256,7 @@
     counts = [min(n, pt - v * n) for v in range(pu)]
     peers = [partner(me, k) for k in range(n)]
     table = origin_table(m)
+    last = m - 2
 
     def pick(place, values):
         total = jnp.int32(0)
@@ -269,6 +271,12 @@
         return total
 
     origins = [by_place([table[z][i] for z in range(m)]) for i in range(m - 1)]
+
+    def when(needed, act):
+        if needed is None:
+            act()
+        else:
+            pl.when(needed)(act)
 
     def describe(src, dst, send, recv, device):
         return pltpu.make_async_remote_copy(
@@ -280,17 +288,35 @@
             device_id_type=MESH,
         )
 
-    waits = []
-
     def remote(src, dst, send, recv, device, needed=None):
         copy = describe(src, dst, send, recv, device)
-        if needed is None:
-            copy.start()
-        else:
-            pl.when(needed)(copy.start)
-        waits.append((copy, needed))
+        when(needed, copy.start)
         return copy
 
+    sent = []
+
+    def drain():
+        while sent:
+            copy, needed = sent.pop(0)
+            when(needed, copy.wait_send)
+
+    barrier = pltpu.get_barrier_semaphore()
+    for z in range(m):
+        for k in range(n):
+            far = lax.rem(t + z, m)
+            if z or k:
+                pl.semaphore_signal(
+                    barrier, inc=1, device_id=(peers[k], far), device_id_type=MESH
+                )
+
+    inputs = []
+    for i, (src, dst) in enumerate((
+        (text_hbm, text_ref), (prompts_hbm, prompts_ref), (cot_hbm, cot_ref),
+        (gain_hbm, gain_ref), (cos_hbm, cos_ref), (sin_hbm, sin_ref),
+    )):
+        load = pltpu.make_async_copy(src, dst, semi.at[i])
+        load.start()
+        inputs.append(load)
     loads = []
     for i, hbm in enumerate((wq_hbm, wk_hbm, wv_hbm)):
         for g in range(per):
@@ -301,127 +327,205 @@
             load.start()
             loads.append(load)
 
-    barrier = pltpu.get_barrier_semaphore()
-    for z in range(m):
-        for k in range(n):
-            far = lax.rem(t + z, m)
-            if z or k:
-                pl.semaphore_signal(
-                    barrier, inc=1, device_id=(peers[k], far), device_id_type=MESH
-                )
-
+    inputs[0].wait()
+    for u in range(tu):
+        if u == 0:
+            tz[t, me] = text_ref[0, me]
+        else:
+            trecv[u - 1, me] = text_ref[u, me]
+    inputs[1].wait()
     whole = p_len // TILE
-    pbuf[:whole] = prompts_ref[: whole * TILE].reshape(whole, TILE, width)
+    spare = pu * n - pt
+    for v in range(pu):
+        full_tiles = max(0, min(n, whole - v * n))
+        if full_tiles:
+            pbuf[v, :full_tiles] = prompts_ref[
+                v * n * TILE : (v * n + full_tiles) * TILE
+            ].reshape(full_tiles, TILE, width)
     if p_len % TILE:
         rest = prompts_ref[whole * TILE : p_len].astype(f32)
         fill = jnp.zeros((TILE - p_len % TILE, width), f32)
-        pbuf[whole] = jnp.concatenate([rest, fill], axis=0).astype(bf16)
-    if pu * n > pt:
-        pbuf[pt:] = jnp.zeros((pu * n - pt, TILE, width), bf16)
+        pbuf[whole // n, whole % n] = jnp.concatenate([rest, fill], axis=0).astype(bf16)
+    if spare:
+        pbuf[pu - 1, n - spare :] = jnp.zeros((spare, TILE, width), bf16)
+    pl.semaphore_wait(barrier, n * m - 1)
+
+    for k in range(1, n):
+        remote(
+            text_ref.at[0, peers[k]], tz.at[t, me], sem_t.at[0, 0], sem_t.at[1, 0],
+            (peers[k], t),
+        )
+    for k in range(1, n):
+        remote(
+            text_ref.at[1:, peers[k]], trecv.at[:, me], sem_t.at[0, 1], sem_t.at[1, 1],
+            (peers[k], t),
+        )
+    for k in range(1, n):
+        remote(
+            pbuf.at[:, peers[k]], precv.at[:, me], sem_p.at[0], sem_p.at[1], (peers[k], t)
+        )
+    spread_0 = describe(
+        text_ref.at[0, 1:], tz.at[t, 1:n], sem_t.at[0, 0], sem_t.at[1, 0], (peers[1], t)
+    )
+    spread_t = describe(
+        text_ref.at[1:, 1:], trecv.at[:, 1:], sem_t.at[0, 1], sem_t.at[1, 1], (peers[1], t)
+    )
+    spread_p = describe(
+        pbuf.at[:, 1:], precv.at[:, 1:], sem_p.at[0], sem_p.at[1], (peers[1], t)
+    )
+    sent += [(spread_0, None), (spread_t, None), (spread_p, None)]
+    for v in range(pu):
+        precv[v, me] = pbuf[v, me]
+    inputs[2].wait()
     cot_pad[:lead] = cot_ref[:lead]
     cot_pad[lead:] = cot_ref[p_len:].astype(f32).astype(bf16)
-    pl.semaphore_wait(barrier, n * m - 1)
-
-    spread_0, spread_t, spread_p = [], [], []
-    for k in range(1, n):
-        spread_0.append(
-            remote(
-                text_ref.at[0, peers[k]], tz.at[t, 0, me],
-                sem_t.at[0, 0, k], sem_t.at[1, 0, k], (peers[k], t),
-            )
-        )
-    for k in range(1, n):
-        if tu > 1:
-            spread_t.append(
-                remote(
-                    text_ref.at[1:, peers[k]], tz.at[t, 1:, me],
-                    sem_t.at[0, 1, k], sem_t.at[1, 1, k], (peers[k], t),
-                )
-            )
-    for k in range(1, n):
-        for v in range(pu):
-            spread_p.append(
-                remote(
-                    pbuf.at[v * n + peers[k]], precv.at[v, me],
-                    sem_p.at[0, v, k], sem_p.at[1, v, k], (peers[k], t),
-                )
-            )
+    sources = [pick(peers[k], lambda e: e) for k in range(n)]
+    tasks_of = [pick(peers[k], lambda e: task_ref[e]) for k in range(n)]
+
+    packed = slots < tu * n
+    rank, ahead = [[jnp.int32(e) for e in range(n)]], jnp.int32(n)
+    for u in range(1, tu):
+        rank.append([])
+        for e in range(n):
+            live_tile = length_ref[e] > u * n * TILE
+            rank[u].append(jnp.where(live_tile, ahead, -1) if packed else jnp.int32(u * n + e))
+            ahead = ahead + jnp.where(live_tile, 1, 0)
+    places = [
+        [pick(peers[k], lambda e: jnp.maximum(rank[u][e], 0)) for k in range(n)]
+        for u in range(tu)
+    ]
+    pieces = [(lo, min(lo + n, slots)) for lo in range(0, slots, n)]
+    ready = {}
     for u in range(tu):
-        tz[t, u, me] = text_ref[u, me]
-    for v in range(pu):
-        precv[v, me] = pbuf[v * n + me]
+        ready.setdefault(min(u, len(pieces) - 1), []).append(u)
 
     ways = [(t < m - 1, lax.rem(t + 1, m)), (t > 0, lax.rem(t + m - 1, m))]
 
     def text_unit(z, g):
-        return tz.at[z, g]
+        lo, hi = pieces[g]
+        return tz.at[z, lo:hi]
 
     def prompt_unit(z, v):
         return fullp.at[z, v, : counts[v]]
 
-    units = [(text_unit, g) for g in range(tu)] + [(prompt_unit, v) for v in range(pu)]
+    units = [(text_unit, g) for g in range(len(pieces))] + [(prompt_unit, v) for v in range(pu)]
+    own_sent = []
 
     def pass_own(i):
         ref = units[i][0](t, units[i][1])
         for w, (needed, far) in enumerate(ways):
-            remote(ref, ref, semz_own.at[w, i], semz_in.at[t, i], (me, far), needed)
-
-    for copy in spread_0:
-        copy.wait_recv()
+            copy = remote(ref, ref, semz_own.at[w, i], semz_in.at[t, i], (me, far), needed)
+            own_sent.append((copy, needed))
+
+    spread_0.wait_recv()
     pass_own(0)
-    for copy in spread_t:
-        copy.wait_recv()
-    for g in range(1, tu):
+    spread_t.wait_recv()
+    for g in range(1, len(pieces)):
+        for i in range(*pieces[g]):
+            if packed:
+                spot = jnp.int32(0)
+                for u in range(1, tu):
+                    for e in range(n):
+                        spot = jnp.where(rank[u][e] == i, (u - 1) * n + e, spot)
+                tz[t, i] = trecv[spot // n, lax.rem(spot, n)]
+            else:
+                tz[t, i] = trecv[i // n - 1, i % n]
         pass_own(g)
 
-    sources = [pick(peers[k], lambda e: e) for k in range(n)]
-    tasks_of = [pick(peers[k], lambda e: task_ref[e]) for k in range(n)]
-
-    for copy in spread_p:
-        copy.wait_recv()
-    collect_p = []
+    spread_p.wait_recv()
     for k in range(1, n):
         for v in range(pu):
             psend[k, v] = precv[v, tasks_of[k]]
-        collect_p.append(
-            remote(
-                psend.at[k], fullp.at[t, :, me], sem_c.at[0, k], sem_c.at[1, k], (peers[k], t)
-            )
-        )
+        remote(psend.at[k], fullp.at[t, :, me], sem_c.at[0], sem_c.at[1], (peers[k], t))
     for v in range(pu):
         fullp[t, v, me] = precv[v, tasks_of[0]]
+    collect_p = describe(
+        psend.at[1:], fullp.at[t, :, 1:], sem_c.at[0], sem_c.at[1], (peers[1], t)
+    )
+    sent.append((collect_p, None))
     collected = {}
 
     def collect(i, z, lo, hi):
-        for u in range(lo, hi):
-            stage[u - lo] = tz[z, u]
         for k in range(1, n):
             for u in range(lo, hi):
-                tsend[i, k, u] = stage[u - lo, sources[k]]
-            collected[i, lo, k] = remote(
+                tsend[i, k, u] = stage[places[u][k]]
+            remote(
                 tsend.at[i, k, lo:hi], fullt.at[z, lo:hi, me],
-                sem_s.at[0, i, lo, k], sem_s.at[1, i, lo, k], (peers[k], t),
+                sem_s.at[0, i, lo], sem_s.at[1, i, lo], (peers[k], t),
             )
         for u in range(lo, hi):
-            fullt[z, u, me] = stage[u - lo, sources[0]]
+            fullt[z, u, me] = stage[places[u][0]]
+        copy = describe(
+            tsend.at[i, 1:, lo:hi], fullt.at[z, lo:hi, 1:],
+            sem_s.at[0, i, lo], sem_s.at[1, i, lo], (peers[1], t),
+        )
+        collected[i, lo] = copy
+        sent.append((copy, None))
 
     def finish(i):
         for key, copy in collected.items():
             if key[0] == i:
                 copy.wait_recv()
 
+    stage[...] = tz[t]
     collect(m - 1, t, 0, tu)
-    for copy in collect_p:
-        copy.wait_recv()
+    collect_p.wait_recv()
     for v in range(pu):
-        pass_own(tu + v)
+        pass_own(len(pieces) + v)
+
+    def take(z, lo, hi):
+        parts = []
+        if lo < lead:
+            parts.append(fullp[z].reshape(pu * n * TILE, width)[lo : min(hi, lead)])
+        if hi > lead:
+            parts.append(fullt[z].reshape(seq, width)[max(lo, lead) - lead : hi - lead])
+        return parts[0] if len(parts) == 1 else jnp.concatenate(parts, axis=0)
+
+    def project(z, fresh, lo=0, hi=rows):
+        wide = take(z, lo, hi).astype(f32)
+        normed = (wide * inv_ref[lo:hi, :1] * gain_ref[z]).astype(bf16)
+        deep = pl.ds(pl.multiple_of(z * width, width), width)
+
+        def body(c, carry):
+            for h in range(inner):
+                b = c * inner + h
+                product = dot_nn(normed, w_ref[b, deep, :])
+                qkv[b, lo:hi] = product if fresh else qkv[b, lo:hi] + product
+            return carry
+
+        inner = blocks if lo or hi < rows else 3
+        if inner == blocks:
+            body(0, 0)
+        else:
+            lax.fori_loop(0, blocks // inner, body, 0)
+
+    due = []
+
+    def pump(i, lo, hi, step):
+        z = origins[i]
+        left = z < t
+        needed = (left & (t < m - 1)) | (jnp.logical_not(left) & (t > 0))
+        far = jnp.where(needed, jnp.where(left, t + 1, t - 1), z)
+        for j in range(lo, hi):
+            ref = units[j][0](z, units[j][1])
+            copy = describe(ref, ref, semz_fwd.at[i, j], semz_in.at[z, j], (me, far))
+            copy.wait_recv()
+            when(needed, copy.start)
+            sent.append((copy, needed))
+            if j < len(pieces):
+                lo_s, hi_s = pieces[j]
+                stage[lo_s:hi_s] = tz[z, lo_s:hi_s]
+                due.extend(ready.get(j, []))
+                if due and (len(due) >= step or j == len(pieces) - 1):
+                    collect(i, z, due[0], due[-1] + 1)
+                    due.clear()
+
+    half = len(pieces) // 2
+    final = len(units)
+    if m > 2:
+        pump(0, 0, final, 2)
     finish(m - 1)
-
-    def whole_rows(z):
-        prompt = fullp[z].reshape(pu * n * TILE, width)[:lead]
-        return jnp.concatenate([prompt, fullt[z].reshape(seq, width)], axis=0)
-
-    own = whole_rows(t).astype(f32)
+    own = take(t, 0, rows).astype(f32)
     square = jnp.broadcast_to(jnp.sum(own * own, axis=1, keepdims=True), (rows, 128))
     padded = squares.shape[2]
     square = jnp.concatenate([square, jnp.zeros((padded - rows, 128), f32)], axis=0)
@@ -434,48 +538,33 @@
                 (me, lax.rem(t + k, m)),
             )
         )
-
-    def project(z, fresh):
-        wide = whole_rows(z).astype(f32)
-        normed = (wide * inv_ref[:, :1] * gain_ref[z]).astype(bf16)
-        deep = pl.ds(pl.multiple_of(z * width, width), width)
-
-        def body(b, carry):
-            product = dot_nn(normed, w_ref[b, deep, :])
-            qkv[b] = product if fresh else qkv[b] + product
-            return carry
-
-        lax.fori_loop(0, blocks, body, 0)
-
-    def receive(i):
-        z = origins[i]
-        left = z < t
-        needed = (left & (t < m - 1)) | (jnp.logical_not(left) & (t > 0))
-        far = jnp.where(needed, jnp.where(left, t + 1, t - 1), z)
-        step = 1 if i == m - 2 else max(1, tu // 2)
-        for j, (unit, g) in enumerate(units):
-            ref = unit(z, g)
-            describe(ref, ref, semz_fwd.at[i, j], semz_in.at[z, j], (me, far)).wait_recv()
-            remote(ref, ref, semz_fwd.at[i, j], semz_in.at[z, j], (me, far), needed)
-            if j < tu and (j + 1) % step == 0:
-                collect(i, z, j + 1 - step, j + 1)
-        finish(i)
-
-    receive(0)
+    for i in range(1, last):
+        pump(i, 0, final, 2)
+    for load in inputs[3:] + loads:
+        load.wait()
     for copy in shared:
         copy.wait_recv()
+        sent.append((copy, None))
     square = squares[0]
     for k in range(1, m):
         square = square + squares[k]
     square = jnp.broadcast_to(square[:1], (128, padded)).T[:rows]
     inv_ref[...] = lax.rsqrt(square * (1.0 / model_width) + 1e-05)
-    for load in loads:
-        load.wait()
     project(t, True)
-    project(origins[0], False)
-    for i in range(1, m - 1):
-        receive(i)
+    if m > 2:
+        finish(0)
+        project(origins[0], False)
+    pump(last, 0, half, 1)
+    for i in range(1, last):
+        finish(i)
         project(origins[i], False)
+    pump(last, half, len(pieces), 1)
+    sent += own_sent
+    drain()
+    finish(last)
+    project(origins[last], False, lead, rows)
+    pump(last, len(pieces), final, 1)
+    project(origins[last], False, 0, lead)
 
     limit = p_len + pick(me, lambda e: length_ref[e])
     scale = 1.0 / math.sqrt(HD)
@@ -504,7 +593,9 @@
             weights = jnp.exp(scores - peak)
             probs = weights * (1.0 / jnp.sum(weights, axis=1, keepdims=True))
             low = probs.astype(bf16)
-            out_ref[:, far] = jnp.where(live, dot_nn(low, v), 0.0).astype(bf16)
+            mixed = jnp.where(live, dot_nn(low, v), 0.0)
+            mixed = jnp.concatenate([mixed[:p_len], mixed[lead:]], axis=0)
+            out_ref[:, far] = mixed.astype(bf16)
             upstream = jnp.where(live, cot_pad[:, far].astype(f32), 0.0).astype(bf16)
             grad_prob = dot_nt(upstream, v)
             delta = jnp.sum(probs * grad_prob, axis=1, keepdims=True)
@@ -530,50 +621,41 @@
     def holds(v, at):
         return None if counts[v] == n else v * n + at < pt
 
-    def when(needed, act):
-        if needed is None:
-            act()
-        else:
-            pl.when(needed)(act)
-
     for i in range(m):
-        z = origins[m - 2 - i] if i < m - 1 else t
+        z = origins[last - i] if i <= last else t
         deep = pl.ds(pl.multiple_of(z * width, width), width)
         total = dot_nt(grads[0], w_ref[0, deep, :])
         for b in range(1, blocks):
             total = total + dot_nt(grads[b], w_ref[b, deep, :])
         prompt = fullp[z].reshape(pu * n * TILE, width)[:lead].astype(f32)
         value = inv * (total * gain_ref[z]) - prompt * factor
-        part[i, :pt] = value.astype(bf16).reshape(pt, TILE, width)
-        for k in range(n):
-            for v in range(pu):
-                if i == m - 1 and k == 0:
+        value = value.astype(bf16).reshape(pt, TILE, width)
+        for v in range(pu):
+            part[i, v, : counts[v]] = value[v * n : v * n + counts[v]]
+        for v in range(pu):
+            for k in range(counts[v]):
+                j = peers[k] if counts[v] == n else k
+                away = None if i <= last else j != me
+                if i > last and counts[v] == n and k == 0:
                     continue
-                remote(
-                    part.at[i, v * n + peers[k]], pin.at[v, me, t],
-                    semg.at[i, v, k], semg_in.at[v, k, t], (peers[k], z), holds(v, peers[k]),
+                copy = remote(
+                    part.at[i, v, j], pin.at[v, me, t], semg.at[i, v, k], semg_in.at[v], (j, z), away
                 )
-        if i == m - 1:
-            for v in range(pu):
-
-                def keep(v=v):
-                    pin[v, me, t] = part[m - 1, v * n + me]
-
-                when(holds(v, me), keep)
+                sent.append((copy, away))
+    homes = []
+    for v in range(pu):
+        home = pltpu.make_async_copy(part.at[m - 1, v, me], pin.at[v, me, t], semg_in.at[v])
+        when(holds(v, me), home.start)
 
     tasks = [pick(s, lambda e: task_ref[e]) for s in range(n)]
     fourth = {}
     for v in range(pu):
 
         def gather(v=v):
-            for k in range(n):
-                for z in range(m):
-                    spot = lax.rem(t + z, m)
-                    if k or z:
-                        describe(
-                            pin.at[v, peers[k], spot], pin.at[v, peers[k], spot],
-                            semg.at[0, v, k], semg_in.at[v, k, spot], (peers[k], spot),
-                        ).wait_recv()
+            describe(
+                pin.at[v], pin.at[v], semg.at[0, v, 0], semg_in.at[v], (peers[1], t)
+            ).wait_recv()
+            sums = [None] * n
             for s in range(n):
                 total = pin[v, s, 0].astype(f32)
                 for z in range(1, m):
@@ -587,22 +669,25 @@
                 else:
                     send4[v, k] = sums[k].astype(bf16)
 
-        sums = [None] * n
         when(holds(v, me), gather)
         for k in range(1, n):
             fourth[v, k] = remote(
                 send4.at[v, k], gout.at[v, me], sem4.at[0, v, k], sem4.at[1, v, k],
                 (peers[k], t), holds(v, me),
             )
+            sent.append((fourth[v, k], holds(v, me)))
     for v in range(pu):
         for k in range(1, n):
             when(holds(v, peers[k]), fourth[v, k].wait_recv)
-        grad_ref[v * n : v * n + counts[v]] = gout[v, : counts[v]]
-    for copy, needed in waits:
-        when(needed, copy.wait_send)
-
-
-def fast_device(text, prompts, gain, w_query, w_key, w_value, cotangent, task_of, lengths, slot):
+    for v in range(pu):
+        for j in range(counts[v]):
+            at = (v * n + j) * TILE
+            size = min(TILE, p_len - at)
+            grad_ref[at : at + size] = gout[v, j].astype(f32)[:size].reshape(size, 1, width)
+    drain()
+
+
+def fast_device(slots, number, text, prompts, gain, w_query, w_key, w_value, cotangent, task_of, lengths, slot):
     n, m = lax.axis_size("dp"), lax.axis_size("tensor")
     f32, bf16 = jnp.float32, jnp.bfloat16
     seq, width = text.shape[1], text.shape[2]
@@ -616,33 +701,39 @@
     row = np.arange(rows)
     pos = np.where(row < lead, np.where(row < p_len, row, 0), row - (lead - p_len))
     half = HD // 2
-    frequency = 10000.0 ** (-jnp.arange(half, dtype=f32) / half)
-    angle = jnp.asarray(pos.astype(np.int32)).astype(f32)[:, None] * frequency[None, :]
-    cosine = jnp.concatenate([jnp.cos(angle)] * 2, axis=1)
-    sine = jnp.concatenate([-jnp.sin(angle), jnp.sin(angle)], axis=1)
+    angle = pos[:, None] * 10000.0 ** (-np.arange(half) / half)[None, :]
+    cosine = np.concatenate([np.cos(angle)] * 2, axis=1).astype(np.float32)
+    sine = np.concatenate([-np.sin(angle), np.sin(angle)], axis=1).astype(np.float32)
     group = 2 * HD if heads % (2 * HD) == 0 else HD
     blocks = 3 * (heads // group)
-    units = tu + pu
+    units = -(-slots // n) + pu
     smem = pl.BlockSpec(memory_space=pltpu.SMEM)
     vmem = pl.BlockSpec(memory_space=pltpu.VMEM)
     hbm = pl.BlockSpec(memory_space=pl.ANY)
     dma = pltpu.SemaphoreType.DMA
     out, collected = pl.pallas_call(
-        functools.partial(step_kernel, p_len),
+        functools.partial(step_kernel, p_len, slots),
         out_shape=(
-            jax.ShapeDtypeStruct((rows, heads), bf16),
-            jax.ShapeDtypeStruct((pt, TILE, width), bf16),
+            jax.ShapeDtypeStruct((p_len + seq, heads), bf16),
+            jax.ShapeDtypeStruct((p_len, 1, width), f32),
         ),
-        in_specs=[smem] * 3 + [vmem] * 6 + [hbm] * 3,
+        in_specs=[smem] * 3 + [hbm] * 9,
         out_specs=(vmem, vmem),
         scratch_shapes=[
             pltpu.VMEM((blocks, m * width, group), bf16),
-            pltpu.VMEM((pu * n, TILE, width), bf16),
+            pltpu.VMEM((tu, n, TILE, width), bf16),
+            pltpu.VMEM((p_len, width), bf16),
+            pltpu.VMEM((m, 1, width), f32),
+            pltpu.VMEM((rows, HD), f32),
+            pltpu.VMEM((rows, HD), f32),
+            pltpu.VMEM((p_len + seq, heads), bf16),
+            pltpu.VMEM((pu, n, TILE, width), bf16),
             pltpu.VMEM((pu, n, TILE, width), bf16),
             pltpu.VMEM((n, pu, TILE, width), bf16),
             pltpu.VMEM((m, pu, n, TILE, width), bf16),
-            pltpu.VMEM((m, tu, n, TILE, width), bf16),
-            pltpu.VMEM((tu, n, TILE, width), bf16),
+            pltpu.VMEM((tu - 1, n, TILE, width), bf16),
+            pltpu.VMEM((m, slots, TILE, width), bf16),
+            pltpu.VMEM((slots, TILE, width), bf16),
             pltpu.VMEM((m, n, tu, TILE, width), bf16),
             pltpu.VMEM((m, tu, n, TILE, width), bf16),
             pltpu.VMEM((m, 8, -(-rows // 128) * 128), f32),
@@ -650,33 +741,49 @@
             pltpu.VMEM((blocks, lead, group), bf16),
             pltpu.VMEM((rows, 128), f32),
             pltpu.VMEM((rows, heads), bf16),
-            pltpu.VMEM((m, pu * n, TILE, width), bf16),
+            pltpu.VMEM((m, pu, n, TILE, width), bf16),
             pltpu.VMEM((pu, n, m, TILE, width), bf16),
             pltpu.VMEM((pu, n, TILE, width), bf16),
             pltpu.VMEM((pu, n, TILE, width), bf16),
             dma((blocks,)),
-            dma((2, 2, n)),
-            dma((2, pu, n)),
-            dma((2, n)),
-            dma((2, m, tu, n)),
+            dma((6,)),
+            dma((2, 2)),
+            dma((2,)),
+            dma((2,)),
+            dma((2, m, tu)),
             dma((2, units)),
             dma((m, units)),
             dma((m, units)),
             dma((2, m)),
             dma((m, pu, n)),
-            dma((pu, n, m)),
+            dma((pu,)),
             dma((2, pu, n)),
         ],
         compiler_params=pltpu.CompilerParams(
-            collective_id=0, has_side_effects=True, vmem_limit_bytes=63 * 2**20
+            collective_id=number, has_side_effects=True, vmem_limit_bytes=63 * 2**20
         ),
     )(
         slot, task_of, lengths, text.reshape(tu, n, TILE, width), prompts[0],
-        gain.reshape(m, 1, width), cosine, sine, cotangent[0], w_query, w_key, w_value,
-    )
-    prompt_grad = collected.reshape(lead, width)[:p_len].astype(f32)[None]
-    attn_out = jnp.concatenate([out[:p_len], out[lead:]], axis=0)[None]
-    return (attn_out, prompt_grad)
+        gain.reshape(m, 1, width), jnp.asarray(cosine), jnp.asarray(sine), cotangent[0],
+        w_query, w_key, w_value,
+    )
+    return (out[None], collected.reshape(1, p_len, width))
+
+
+def fast_path(text, prompts, gain, w_query, w_key, w_value, cotangent, task_of, lengths, slot):
+    n = lax.axis_size("dp")
+    granule = TILE * n
+    tiles = text.shape[1] // granule
+    every = n * tiles
+    few = every * 3 // 4
+    args = (text, prompts, gain, w_query, w_key, w_value, cotangent, task_of, lengths, slot)
+    live = jnp.sum((lengths + (granule - 1)) // granule)
+    return lax.cond(
+        live <= few,
+        functools.partial(fast_device, few, 0),
+        functools.partial(fast_device, every, 1),
+        *args,
+    )
 
 
 def choose(text, prompts, *rest):
@@ -685,14 +792,15 @@
     fits = (
         text.shape[0] == 1
         and prompts.shape[0] == 1
-        and m >= 2
+        and m >= 3
         and n >= 2
         and n & (n - 1) == 0
         and n <= 8
+        and seq // (TILE * n) % 4 == 0
         and seq % (TILE * n) == 0
         and text.shape[2] % 128 == 0
     )
-    return (fast_device if fits else on_device)(text, prompts, *rest)
+    return (fast_path if fits else on_device)(text, prompts, *rest)
 
 
 def solution(mesh):

time: 136 us -> 112 us (0.82)
  Pallas kernels: 127 us -> 106 us
  other arithmetic: 4.21 us -> 1.3 us
    pallas_call x1, Pallas kernels: 127 us -> 106 us  [fast_device(): pl.pallas_call(functools.partial(step_kernel, p_len, slots), out_shape=(j...]
    unnamed x0 -> x2, local copies, waits for them, and re-layouts: none -> 2.69 us
    slice x2 -> x0, local copies, waits for them, and re-layouts: 1.95 us -> none  [fast_device(): attn_out = jnp.concatenate([out[:p_len], out[lead:]], axis=0)[None]]
    broadcast_in_dim x2 -> x0, other arithmetic: 1.89 us -> none  [the longest x1 0.99 us: fast_device(): prompt_grad = collected.reshape(lead, width)[:p_len].astype(f32)[None]]
    neg x1 -> x0, other arithmetic: 1.4 us -> none  [fast_device(): sine = jnp.concatenate([-jnp.sin(angle), jnp.sin(angle)], axis=1)]
where the time goes in v2:
time: 112 us; the launch traced here: 111 us
  Pallas kernels  106 us (95%)
  local copies, waits for them, and re-layouts  2.69 us (2%)
  other arithmetic  1.3 us (1%)
  between operations  1.29 us (1%)
    pallas_call x1, Pallas kernels, fast_device(): pl.pallas_call(functools.partial(step_kernel, p_len, slots), out_shape=(j...  106 us
    unnamed x2, local copies, waits for them, and re-layouts  2.69 us

profile of v2, /device:TPU:11, one launch (start us, length us, event | category | flops | bytes accessed | tf_op | source)
XLA Modules:
  0.0 111.2 jit_solution(17878605628781573674)
XLA Ops:
  0.6 1.3 %fusion = s32[]{:T(128)} fusion(s32[8]{0:T(128)} %param.24), kind=kLoop, calls=%fused_computation.4 | loop fusion | flops 135 | bytes 36 | tf_op jit(solution)/shard_map/reduce_sum | solution.py:780
  2.6 106.0 %conditional.1 = ((bf16[356,768]{1,0:T(8,128)(2,1)S(1)}, f32[100,1,1280]{2,1,0:T(1,128)})) conditional(s32[]{:T(128)} %convert_element_type.3, (bf16[1,256,1280]{2,1,0:T(8,128)(2,1)}, bf16[1,100,1280]{2,1,0:T(8,128)(2,1)}, f32[5120]{0:T(1024)}, bf16[1,356,768]{2,1,0:T(8,128)(2,1)}, s32[8]{0:T(128)}, /*index=5*/s32[8]{0:T(128)}, s32[8]{0:T(128)}, ...), branch_computations={%region_1.2_spmd, %region_2.3_spmd} | conditional | bytes 8 | solution.py:781
  2.8 105.8 %branch_1_fun.1 = (bf16[356,768]{1,0:T(8,128)(2,1)S(1)}, f32[100,1,1280]{2,1,0:T(1,128)}) custom-call(s32[8]{0:T(128)} %get-tuple-element.62.slot_ref, s32[8]{0:T(128)} %get-tuple-element.63.task_ref, s32[8]{0:T(128)} %get-tuple-element.64.length_ref, bf16[4,8,8,1280]{3,2,1,0:T(8,128)(2,1)} %bitcast.11, bf16[100,1280]{1,0:T(8,128)(2,1)} %bitcast.15, ...), custom_call_target="tpu_custom_call" | custom-call | tf_op jit(solution)/shard_map/cond/branch_1_fun/pallas_call | solution.py:714
  108.5 0.8 copy.22
  109.4 1.9 %copy.23 = f32[1,100,1280]{2,0,1:T(1,128)} copy(f32[1,100,1280]{2,0,1:T(1,128)} %bitcast.17) | data formatting | bytes 1024000
